TPU v7x, 256 devices: a whole 4x4x8 slice. The times are simulated.
256 devices in a mesh: param: 128 (over z, x, y), sensor: 2 (over core).
Axes of the slice: x: 4, y: 4, z: 8, core: 2. Of those that a mesh axis runs over, the one named last changes fastest.
Arguments:
- data: float32 [16, 512, 420], P(None, ('sensor', 'param')), may hold values from -6 to 6
- spectra: float32 [2, 512, 512, 421], P(None, 'sensor', 'param'), may hold values from -2 to 2
Outputs:
- gradient: float32 [16, 512, 420], P(None, 'param')
- rms: float32 [16], replicated
All inputs are finite; a program needn't handle non-finite values.
Results may differ from a plain program's by a relative error of at most 0.0003.
Values sent between devices are 32-bit elements; how exact they have to be, the bound alone decides.
A program may use at most 128 MiB of HBM per device.

v0:
```python
import math

import jax
import jax.numpy as jnp
from jax import lax
from jax.sharding import Mesh
from jax.sharding import PartitionSpec as P

PARAM = ("param_0", "param_1", "param_2")
SENSOR_PARAM = ("sensor", "param_0", "param_1", "param_2")


def copy_for_each(array, axis):
    copies = jnp.broadcast_to(array, (lax.axis_size(axis), *array.shape))
    return lax.all_to_all(copies, axis, split_axis=0, concat_axis=0, tiled=True)


def of_everyone(array, axis):
    return copy_for_each(array, axis).sum(axis=0)


def by_axis(array, axes):
    for axis in axes:
        array = lax.psum(array, axis)
    return array


def spectral_tables(steps):
    length = 2 * steps
    freqs = steps + 1
    times = lax.broadcasted_iota(jnp.int32, (steps, freqs), 0)
    bins = lax.broadcasted_iota(jnp.int32, (steps, freqs), 1)
    phase = 2.0 * math.pi / length * (times * bins % length).astype(jnp.float32)
    forward = jnp.concatenate([jnp.cos(phase), -jnp.sin(phase)], axis=1)
    weight = jnp.where((bins == 0) | (bins == steps), 1.0, 2.0) / length
    backward = jnp.concatenate([(weight * jnp.cos(phase)).T, (-weight * jnp.sin(phase)).T], axis=0)
    return (forward, backward)


def to_spectrum(series, forward):
    vectors, sensors, steps = series.shape
    flat = jnp.dot(
        series.reshape(vectors * sensors, steps),
        forward,
        precision=lax.Precision.HIGHEST,
        preferred_element_type=jnp.float32,
    )
    return flat.reshape(vectors, sensors, forward.shape[1])


def contract(kernel, spectrum):
    return jnp.einsum(
        "spf,rsf->rpf",
        kernel,
        spectrum,
        precision=lax.Precision.HIGHEST,
        preferred_element_type=jnp.float32,
    )


def body(data, spectra):
    steps = data.shape[2]
    freqs = steps + 1
    forward, backward = spectral_tables(steps)
    whole = lax.all_gather(to_spectrum(data, forward), PARAM, axis=1, tiled=True)
    real_part = whole[..., :freqs]
    imag_part = whole[..., freqs:]
    kernel_re = spectra[0]
    kernel_im = spectra[1]
    out_re = contract(kernel_re, real_part) + contract(kernel_im, imag_part)
    out_im = contract(kernel_re, imag_part) - contract(kernel_im, real_part)
    vectors, points = (out_re.shape[0], out_re.shape[1])
    stacked = jnp.concatenate([out_re, out_im], axis=2).reshape(vectors * points, 2 * freqs)
    partial_field = jnp.dot(
        stacked, backward, precision=lax.Precision.HIGHEST, preferred_element_type=jnp.float32
    ).reshape(vectors, points, steps)
    count = points * lax.axis_size(PARAM) * steps
    summed = of_everyone(partial_field, "sensor")
    squares = by_axis(jnp.sum(summed * summed, axis=(1, 2)), PARAM)
    scale = jnp.sqrt(squares / count + 1e-06)
    return (summed / scale[:, None, None], scale)


def solution(mesh):
    split = Mesh(
        mesh.devices.reshape(8, 4, 4, mesh.shape["sensor"]),
        ("param_0", "param_1", "param_2", "sensor"),
    )
    placed = (P(None, SENSOR_PARAM, None), P(None, "sensor", PARAM, None))
    return jax.shard_map(
        body, mesh=split, in_specs=placed, out_specs=(P(None, PARAM, None), P()), check_vma=False
    )
```

profile of v0, /device:TPU:2, one launch (start us, length us, event | category | flops | bytes accessed | tf_op | source)
XLA Modules:
  0.0 276.1 jit_solution(3874068766447296072)
XLA Ops:
  7.2 3.6 %sine_negate_fusion = (f32[420,421]{1,0:T(8,128)S(1)}, f32[420,421]{1,0:T(8,128)S(1)}) fusion(), kind=kLoop, calls=%fused_computation.36 | loop fusion | flops 1768200 | bytes 1414560 | tf_op jit(solution)/shard_map/neg | solution.py:34
  10.8 0.9 reshape.15
  11.7 1.1 fusion.31
  12.8 0.1 reshape.16
  12.9 0.7 copy.12
  13.6 4.6 %sine_multiply_fusion = (f32[421,420]{0,1:T(8,128)}, f32[421,420]{0,1:T(8,128)}) fusion(f32[421]{0:T(512)S(1)} %fusion.49, f32[421]{0:T(512)S(1)} %select_multiply_fusion), kind=kLoop, calls=%fused_computation.31 | loop fusion | flops 1945020 | bytes 1417928 | tf_op jit(solution)/shard_map/mul | solution.py:36
  18.2 141.5 %all-gather.2.cloned.1.call-done = f32[16,256,842]{2,0,1:T(8,128)} async-done(((f32[16,2,842]{2,0,1:T(8,128)}), f32[16,256,842]{2,0,1:T(8,128)}) %all-gather.2.cloned.1.call-update) | async-done | bytes 13795344 | tf_op jit(solution)/shard_map/all_gather | solution.py:65
  159.7 11.1 %fusion.52 = (f32[16,256,421]{2,0,1:T(8,128)}, f32[16,256,421]{2,0,1:T(8,128)}) fusion(f32[16,256,842]{2,0,1:T(8,128)} %all-gather.2.cloned.1.call-done), kind=kLoop, calls=%fused_computation.56 | loop fusion | bytes 27590656 | tf_op jit(solution)/shard_map/slice | solution.py:67
  170.8 10.2 %copy.19 = f32[16,256,421]{1,0,2:T(8,128)} copy(f32[16,256,421]{2,0,1:T(8,128)} %get-tuple-element.6) | data formatting | bytes 13795328
  181.0 10.4 %copy.18 = f32[16,256,421]{1,0,2:T(8,128)} copy(f32[16,256,421]{2,0,1:T(8,128)} %get-tuple-element.7) | data formatting | bytes 13795328
  191.4 8.5 %fusion.2 = f32[421,16,4]{1,2,0:T(4,128)S(1)} fusion(f32[16,256,421]{1,0,2:T(8,128)} %copy.19, f32[2,256,4,421]{1,2,3,0:T(4,128)S(1)} %copy-done.1), kind=kOutput, calls=%fused_computation.2 | convolution fusion | flops 82771968 | bytes 8729856 | tf_op jit(solution)/shard_map/spf,rsf->rpf/dot_general | solution.py:52
  200.0 7.0 %fusion = f32[421,16,4]{1,2,0:T(4,128)} fusion(f32[16,256,421]{1,0,2:T(8,128)S(1)} %copy-done, f32[2,256,4,421]{1,2,3,0:T(4,128)S(1)} %copy-done.1), kind=kOutput, calls=%fused_computation | convolution fusion | flops 82771968 | bytes 8729856 | tf_op jit(solution)/shard_map/spf,rsf->rpf/dot_general | solution.py:52
  207.0 7.3 %fusion.22 = f32[16,4,421]{0,1,2:T(4,128)} fusion(f32[421,16,4]{1,2,0:T(4,128)S(1)} %fusion.2, f32[16,256,421]{1,0,2:T(8,128)S(1)} %copy-done, f32[2,256,4,421]{1,2,3,0:T(4,128)S(1)} %copy-done.1), kind=kOutput, calls=%fused_computation.21 | convolution fusion | flops 82798912 | bytes 9592064 | tf_op jit(solution)/shard_map/spf,rsf->rpf/dot_general | solution.py:52
  214.3 2.1 copy.15
  216.4 9.0 %fusion.28 = f32[16,4,421]{0,1,2:T(4,128)} fusion(f32[421,16,4]{1,2,0:T(4,128)} %fusion, f32[16,256,421]{1,0,2:T(8,128)} %copy.19, f32[2,256,4,421]{1,2,3,0:T(4,128)S(1)} %copy-done.1), kind=kOutput, calls=%fused_computation.23 | convolution fusion | flops 82798912 | bytes 8837632 | tf_op jit(solution)/shard_map/spf,rsf->rpf/dot_general | solution.py:52
  225.4 1.5 copy.16
  226.9 3.1 %fusion.16 = f32[16,4,420]{2,0,1:T(8,128)S(1)} fusion(f32[421,420]{0,1:T(8,128)} %get-tuple-element.10, f32[421,420]{0,1:T(8,128)} %get-tuple-element.11, f32[16,4,421]{2,0,1:T(8,128)S(1)} %copy.16, f32[16,4,421]{2,0,1:T(8,128)} %copy.15), kind=kOutput, calls=%fused_computation.17 | convolution fusion | flops 272003040 | bytes 1737632 | tf_op jit(solution)/shard_map/dot_general | solution.py:74
  230.0 3.9 %all_to_all.5 = f32[2,16,4,420]{3,1,2,0:T(8,128)S(1)} all-to-all(f32[2,16,4,420]{3,1,2,0:T(8,128)S(1)} %broadcast_in_dim.14), channel_id=1, replica_groups=mesh['param_0'=8,'param_1'=4,'param_2'=4,'sensor'=2] {'sensor'}, dimensions={0} | all-to-all | bytes 430080 | tf_op jit(solution)/shard_map/all_to_all | solution.py:15
  234.0 0.1 multiply_reduce_fusion
  234.1 15.5 %psum.21 = f32[16]{0:T(128)S(1)} all-reduce(f32[16]{0:T(128)S(1)} %multiply_reduce_fusion), channel_id=1, replica_groups=mesh['param_0'=8,'param_1'=4,'param_2'=4,'sensor'=2] {'param_0'}, use_global_device_ids=true, to_apply=%region_2.3 | all-reduce | flops 16 | bytes 128 | tf_op jit(solution)/shard_map/psum | solution.py:24
  249.6 8.6 %psum.22 = f32[16]{0:T(128)S(1)} all-reduce(f32[16]{0:T(128)S(1)} %psum.21), channel_id=1, replica_groups=mesh['param_0'=8,'param_1'=4,'param_2'=4,'sensor'=2] {'param_1'}, use_global_device_ids=true, to_apply=%region_3.4 | all-reduce | flops 16 | bytes 128 | tf_op jit(solution)/shard_map/psum | solution.py:24
  258.2 10.1 %psum.23 = f32[16]{0:T(128)S(1)} all-reduce(f32[16]{0:T(128)S(1)} %psum.22), channel_id=1, replica_groups=mesh['param_0'=8,'param_1'=4,'param_2'=4,'sensor'=2] {'param_2'}, use_global_device_ids=true, to_apply=%region_4.5 | all-reduce | flops 16 | bytes 128 | tf_op jit(solution)/shard_map/psum | solution.py:24
  268.4 0.1 broadcast_divide_fusion
  268.5 0.7 copy.17
  (13 shorter events, 0.1 us)
Async XLA Ops:
  7.2 152.5 %all-gather.2.cloned.1.call-start = ((), (), s32[]{:S(2)}) async-start(), calls=%async_computation.1 | async-start | bytes 14794752 | tf_op jit(solution)/shard_map/all_gather | solution.py:65
  181.0 10.4 %copy-start.1 = (f32[2,256,4,421]{1,2,3,0:T(4,128)S(1)}, f32[2,256,4,421]{1,2,3,0:T(4,128)}, u32[]{:S(2)}) copy-start(f32[2,256,4,421]{1,2,3,0:T(4,128)} %param.3) | copy-start | bytes 10346500
  191.4 8.6 %copy-start = (f32[16,256,421]{1,0,2:T(8,128)S(1)}, f32[16,256,421]{1,0,2:T(8,128)}, u32[]{:S(2)}) copy-start(f32[16,256,421]{1,0,2:T(8,128)} %copy.18) | copy-start | bytes 20692996
  268.4 0.8 copy-start.2
Sparse Core Ops, SparseCore 0:
  13.7 145.9 all-gather.1
where the time goes:
time: 277 us; the launch traced here: 276 us
  waiting for transfers between devices  142 us (51%)
  blocking collectives  38.2 us (14%)
  local copies, waits for them, and re-layouts  37.7 us (14%)
  matrix products  36.1 us (13%)
  between operations  14.1 us (5%)
  other arithmetic  8.45 us (3%)
    all_gather x1, waiting for transfers between devices, body(): lax.all_gather(to_spectrum(data, forward), PARAM, axis=1, tiled=True)  142 us
    psum x3, blocking collectives, by_axis(): array = lax.psum(array, axis)  34.2 us
    dot_general x4, matrix products, contract(): jnp.einsum('spf,rsf->rpf', kernel, spectrum, precision=lax.Precision.HIGH...  31.9 us
    unnamed x9, local copies, waits for them, and re-layouts  21.4 us
    slice x1, local copies, waits for them, and re-layouts, body(): imag_part = whole[..., freqs:]  11.1 us
  transfers between devices with their start and end apart: 1, of which 1 were waited for; matrix products, arithmetic and copies ran while one was open for 2% of the time, Pallas kernels for 0%

commit v1 on v0

v1 whole, which is shorter than its diff:
```python
import functools
import math
import random

import jax
import jax.numpy as jnp
import numpy as np
from jax import lax
from jax.experimental import pallas as pl
from jax.experimental.pallas import tpu as pltpu
from jax.sharding import Mesh
from jax.sharding import PartitionSpec as P

PARAM = ("param_0", "param_1", "param_2")
SENSOR_PARAM = ("sensor", "param_0", "param_1", "param_2")
MESH = pl.DeviceIdType.MESH
F32 = jnp.float32
BF16 = jnp.bfloat16
TORUS = (8, 4, 4)
DIRS = ((0, 1, 0), (0, -1, 0), (0, 0, 1), (0, 0, -1), (1, 0, 0), (-1, 0, 0))
EXTRA = (2, 0, 0)
ROWS = 112
LANES = 128
PIECE = 45
REST = 37
SETUP_STEPS = 4
VMEM_LIMIT = 66_800_000


def moved(offset, step):
    return tuple((a + b) % n for a, b, n in zip(offset, step, TORUS))


def attempt(seed):
    rng = random.Random(seed)
    got = {(0, 0, 0): 0, EXTRA: 2}
    steps = []
    number = (math.prod(TORUS) - 2) // 6
    for k in range(1, number + 1):
        for lag in (3, 2, 1):
            cand = []
            for d in range(6):
                edges = []
                for p, s in got.items():
                    c = moved(p, DIRS[d])
                    if c in got or (s > 0 and s > k - min(lag, max(1, k - 1))):
                        continue
                    edges.append((s, rng.random(), p, c))
                cand.append(sorted(edges))
            used = {}

            def augment(d, seen):
                for s, _, p, c in cand[d]:
                    if c in seen:
                        continue
                    seen.add(c)
                    if c not in used or augment(used[c][0], seen):
                        used[c] = (d, p)
                        return True
                return False

            count = sum(augment(d, set()) for d in sorted(range(6), key=lambda d: len(cand[d])))
            if count == 6:
                break
        else:
            return None
        for c, (d, p) in used.items():
            got[c] = k
        steps.append(sorted((d, p, c) for c, (d, p) in used.items()))
    lags = [k - got[p] for k, step in enumerate(steps, 1) for d, p, c in step if got[p] > 0 and k > 3]
    return (sum(10 ** (3 - lag) for lag in lags if lag < 3), steps)


def make_schedule():
    best = None
    for seed in range(150):
        found = attempt(seed)
        if found and (best is None or found[0] < best[0]):
            best = found
    return best[1]


def spectral_tables(steps):
    half = steps // 2
    t = np.arange(steps)[:, None]
    even = 2 * np.arange(half + 1)[None, :]
    odd = 2 * np.arange(half)[None, :] + 1
    turn = math.pi / steps
    even_re = np.cos(turn * (t * even % (2 * steps)))
    even_im = -np.sin(turn * (t * even % (2 * steps)))
    even_im[:, 0] = np.arange(steps) == 0
    even_im[:, half] = 0.0
    odd_re = np.cos(turn * (t * odd % (2 * steps)))
    odd_im = -np.sin(turn * (t * odd % (2 * steps)))
    forward = np.zeros((512, 512))
    forward[:steps, : half + 1] = even_re
    forward[:steps, 256 : 256 + half + 1] = even_im
    weight = np.full((half + 1,), 2.0 / steps)
    weight[0] = weight[half] = 1.0 / steps
    across = np.zeros((2, 256, 256))
    across[0, : half + 1, :half] = weight[:, None] * (even_re.T @ odd_im)
    across[1, : half + 1, :half] = weight[:, None] * (even_im.T @ odd_re)
    across[1, 0, :half] = 1.0
    gains = np.zeros((8, 512))
    gains[0, : half + 1] = weight / 2
    gains[0, 256 : 256 + half] = 1.0 / steps
    gains[1] = gains[0]
    gains[1, 0] = 0.0
    return (forward, across, gains)


def high_low(array):
    array = array.astype(np.float32)
    high = array.astype(jnp.bfloat16)
    low = (array - high.astype(np.float32)).astype(jnp.bfloat16)
    return (high, low)


def split(value):
    high = value.astype(BF16)
    return (high, (value - high.astype(F32)).astype(BF16))


def times(value, high, low, transposed=False):
    dims = (((1,), (1 if transposed else 0,)), ((), ()))
    dot = functools.partial(lax.dot_general, dimension_numbers=dims, preferred_element_type=F32)
    upper, lower = split(value)
    return dot(upper, high) + dot(lower, high) + dot(upper, low)


def kernel(
    steps,
    data_ref,
    k_ref,
    fh_ref,
    fl_ref,
    ah_ref,
    al_ref,
    gain_ref,
    field_ref,
    rms_ref,
    gat,
    xv,
    xs,
    kraw,
    kt,
    fh,
    fl,
    ah,
    al,
    gain,
    eb,
    do,
    acc,
    part,
    other,
    red1,
    red2,
    srow,
    send_sem,
    recv_sem,
    load_sem,
    pair_sem,
    r1_send,
    r1_recv,
    r2_send,
    r2_recv,
):
    vectors, own, length = data_ref.shape
    me = tuple(lax.axis_index(name) for name in PARAM)
    core = lax.axis_index("sensor")

    def device(offset):
        return {
            name: lax.rem(pos + (o % n), n) for name, pos, o, n in zip(PARAM, me, offset, TORUS)
        }

    partner = {"sensor": 1 - core}
    barrier = pltpu.get_barrier_semaphore()
    for offset in DIRS + (tuple(-o for o in EXTRA),):
        pl.semaphore_signal(barrier, inc=1, device_id=device(offset), device_id_type=MESH)
    pl.semaphore_signal(barrier, inc=1, device_id=partner, device_id_type=MESH)

    rows_k = k_ref.shape[1]
    loads = [
        pltpu.make_async_copy(data_ref, xv, load_sem.at[0]),
        pltpu.make_async_copy(fh_ref, fh, load_sem.at[1]),
        pltpu.make_async_copy(fl_ref, fl, load_sem.at[2]),
        pltpu.make_async_copy(k_ref, kraw.at[:, pl.ds(0, rows_k), :], load_sem.at[3]),
        pltpu.make_async_copy(ah_ref, ah, load_sem.at[4]),
        pltpu.make_async_copy(al_ref, al, load_sem.at[5]),
        pltpu.make_async_copy(gain_ref, gain, load_sem.at[6]),
    ]
    for load in loads:
        load.start()

    slot_of = {(0, 0, 0): 0, EXTRA: 1}
    for k, step in enumerate(steps):
        for i, (d, p, c) in enumerate(step):
            slot_of[c] = 2 + 6 * k + i
    step_of = {c: k for k, step in enumerate(steps, 1) for d, p, c in step}
    step_of[(0, 0, 0)] = 0
    step_of[EXTRA] = 2
    pending = {}
    for k, step in enumerate(steps):
        for d, p, c in step:
            pending.setdefault(step_of[p], []).append((d, p, c))

    def copy(source, target, offset):
        return pltpu.make_async_remote_copy(
            src_ref=gat.at[source],
            dst_ref=gat.at[target],
            send_sem=send_sem.at[target],
            recv_sem=recv_sem.at[target],
            device_id=device(offset),
            device_id_type=MESH,
        )

    def forward_after(k):
        for d, p, c in pending.get(k, ()):
            copy(slot_of[p], slot_of[c], DIRS[d]).start()

    xs[:, pl.ds(384, LANES)] = jnp.zeros((2 * vectors, LANES), F32)
    loads[0].wait()
    for r in range(vectors):
        for s in range(own):
            xs[pl.ds(s * vectors + r, 1), pl.ds(0, length)] = xv[r, pl.ds(s, 1), :]
    loads[1].wait()
    loads[2].wait()
    spec = times(xs[...], fh[...], fl[...])
    lane = lax.broadcasted_iota(jnp.int32, (32, LANES), 1)
    lane8 = lax.broadcasted_iota(jnp.int32, (8, LANES), 1)
    re_b = spec[:, 128:256]
    im_b = spec[:, 384:512]
    gat[0, pl.ds(0, 32), :] = spec[:, 0:128]
    gat[0, pl.ds(32, 32), :] = spec[:, 256:384]
    gat[0, pl.ds(64, 32), :] = re_b + pltpu.roll(
        jnp.where(lane < PIECE, im_b, 0.0), LANES - PIECE, 1
    )
    rest = jnp.where((lane >= PIECE) & (lane < PIECE + REST), im_b, 0.0)
    groups = [
        pltpu.roll(rest[8 * g : 8 * g + 8], (REST * (g % 3) - PIECE) % LANES, 1) for g in range(4)
    ]
    gat[0, pl.ds(96, 8), :] = groups[0] + groups[1] + groups[2]
    gat[0, pl.ds(104, 8), :] = groups[3]

    pl.semaphore_wait(barrier, 8)
    forward_after(0)
    copy(0, 1, EXTRA).start()

    for offset, slot in slot_of.items():
        z, x, y = (
            lax.rem(pos + n - o, n) for pos, o, n in zip(me, offset, TORUS)
        )
        srow[slot] = ((z * TORUS[1] + x) * TORUS[2] + y) * own * 8

    acc[...] = jnp.zeros(acc.shape, F32)
    for c in range(2):
        tail_rows = kraw.shape[1] - rows_k
        kraw[c, pl.ds(rows_k, tail_rows), :] = jnp.zeros((tail_rows, LANES), F32)
    loads[3].wait()
    loads[4].wait()
    loads[5].wait()
    loads[6].wait()

    def transpose_tile(ft):
        parity, half = divmod(ft, 2)
        base = (2 * half * LANES + parity) * 8

        @pl.loop(0, 8)
        def _(i):
            st = i // 4
            p = lax.rem(i, 4)
            for c in range(2):
                block = kraw[c, pl.ds(base + st * 4 + p, LANES, stride=16), :]
                turned = block.T
                if c == 1 and ft == 0:
                    first = lax.broadcasted_iota(jnp.int32, (LANES, LANES), 1) == 0
                    turned = jnp.where(first, 0.0, turned)
                kt[ft, pl.ds(st * LANES * 8 + c * 4 + p, LANES, stride=8), :] = turned

    def wait_slot(slot):
        copy(0, slot, DIRS[0]).wait_recv()

    def consume(first, count):
        number = 32 * count
        for j in range(count):
            tile2 = gat[first + j, pl.ds(64, 32), :]
            left = gat[first + j, pl.ds(96, 16), :]
            moved2 = pltpu.roll(tile2, PIECE, 1)
            for g in range(4):
                source = left[8:16] if g == 3 else left[0:8]
                back = pltpu.roll(source, (PIECE - REST * (g % 3)) % LANES, 1)
                value = jnp.where(
                    lane8 < PIECE,
                    moved2[8 * g : 8 * g + 8],
                    jnp.where(lane8 < PIECE + REST, back, 0.0),
                )
                eb[pl.ds(32 * j + 8 * g, 8), :] = value

        def tiles(row):
            return gat[pl.ds(first, count), pl.ds(row, 32), :].reshape(number, LANES)

        even_re = jnp.concatenate([tiles(0), tiles(64)], axis=1)
        do[pl.ds(0, number), pl.ds(256, 256)] = times(even_re, ah[0], al[0])
        even_im = jnp.concatenate([tiles(32), eb[pl.ds(0, number), :]], axis=1)
        do[pl.ds(0, number), pl.ds(0, 256)] = times(even_im, ah[1], al[1])

        def d_value(ft, j, s, h, imag):
            inner = s * 16 + h * 8
            if ft == 0:
                return gat[first + j, pl.ds((32 if imag else 0) + inner, 8), :]
            if ft == 1:
                if imag:
                    return eb[pl.ds(pl.multiple_of(j * 32 + inner, 8), 8), :]
                return gat[first + j, pl.ds(64 + inner, 8), :]
            return do[
                pl.ds(pl.multiple_of(j * 32 + inner, 8), 8),
                pl.ds((256 if imag else 0) + (ft - 2) * LANES, LANES),
            ]

        for ft in range(4):
            start = tuple(
                acc[c, pl.ds(p * 16 + h * 8, 8), pl.ds(ft * LANES, LANES)]
                for c in range(2)
                for p in range(4)
                for h in range(2)
            )

            def sensors(j, sums):
                sums = list(sums)
                row = srow[first + j]
                for s in range(own):
                    d_re = [d_value(ft, j, s, h, False) for h in range(2)]
                    d_im = [d_value(ft, j, s, h, True) for h in range(2)]
                    for p in range(4):
                        at = pl.multiple_of(row + s * 8, 8)
                        k_re = jnp.broadcast_to(kt[ft, pl.ds(at + p, 1), :], (8, LANES))
                        k_im = jnp.broadcast_to(kt[ft, pl.ds(at + 4 + p, 1), :], (8, LANES))
                        for h in range(2):
                            i = p * 2 + h
                            sums[i] = sums[i] + k_re * d_re[h] + k_im * d_im[h]
                            sums[8 + i] = sums[8 + i] + k_re * d_im[h] - k_im * d_re[h]
                return tuple(sums)

            final = lax.fori_loop(0, count, sensors, start)
            for i, value in enumerate(final):
                c, p, h = i // 8, i // 2 % 4, i % 2
                acc[c, pl.ds(p * 16 + h * 8, 8), pl.ds(ft * LANES, LANES)] = value

    last = len(steps)

    @pl.loop(1, last + 1)
    def _(k):
        for i in range(6):
            wait_slot(2 + 6 * (k - 1) + i)

        @pl.when(k == 2)
        def _():
            wait_slot(1)

        for number in range(1, last):
            if number in pending:

                @pl.when(k == number)
                def _():
                    forward_after(number)

        @pl.when(k <= SETUP_STEPS)
        def _():
            for ft in range(4):

                @pl.when(k == ft + 1)
                def _():
                    transpose_tile(ft)

        @pl.when(k == SETUP_STEPS)
        def _():
            consume(0, 2)

        caught = 2 * SETUP_STEPS
        low = jnp.where(k <= SETUP_STEPS, 0, jnp.where(k <= caught, 2 * (k - SETUP_STEPS) - 2, k - 1))
        high = jnp.where(k <= SETUP_STEPS, 0, jnp.where(k <= caught, 2 * (k - SETUP_STEPS), k))

        @pl.loop(low, high)
        def _(b):
            consume(2 + 6 * b, 6)

    out_re = acc[0] * gain[0:1, :]
    out_im = acc[1] * gain[1:2, :]
    s_re = out_re[:, 0:256] + times(out_im[:, 256:512], ah[0], al[0], True)
    s_im = out_im[:, 0:256] + times(out_re[:, 256:512], ah[1], al[1], True)
    total = times(s_re, fh[:, 0:256], fl[:, 0:256], True) + times(
        s_im, fh[:, 256:512], fl[:, 256:512], True
    )
    part[...] = total
    swap = pltpu.make_async_remote_copy(
        src_ref=part,
        dst_ref=other,
        send_sem=pair_sem.at[0],
        recv_sem=pair_sem.at[1],
        device_id=partner,
        device_id_type=MESH,
    )
    swap.start()
    for slot in range(1, gat.shape[0]):
        copy(0, slot, DIRS[0]).wait_send()
    swap.wait()
    field = part[...] + other[...]
    field_ref[...] = field
    square = field * field
    square = square[:, 0:128] + square[:, 128:256] + square[:, 256:384] + square[:, 384:512]
    square = square[0:16] + square[16:32] + square[32:48] + square[48:64]

    z, x, y = me
    spot = x * TORUS[2] + y
    red1[spot] = square
    sends = []
    for dx in range(TORUS[1]):
        for dy in range(TORUS[2]):
            i = dx * TORUS[2] + dy
            if i == 0:
                continue
            sends.append(
                pltpu.make_async_remote_copy(
                    src_ref=red1.at[spot],
                    dst_ref=red1.at[spot],
                    send_sem=r1_send.at[i],
                    recv_sem=r1_recv.at[i],
                    device_id=device((0, dx, dy)),
                    device_id_type=MESH,
                )
            )
    for send in sends:
        send.start()
    for send in sends:
        send.wait()
    plane = red1[0]
    for i in range(1, TORUS[1] * TORUS[2]):
        plane = plane + red1[i]
    red2[z] = plane
    sends = []
    for dz in range(1, TORUS[0]):
        sends.append(
            pltpu.make_async_remote_copy(
                src_ref=red2.at[z],
                dst_ref=red2.at[z],
                send_sem=r2_send.at[dz],
                recv_sem=r2_recv.at[dz],
                device_id=device((dz, 0, 0)),
                device_id_type=MESH,
            )
        )
    for send in sends:
        send.start()
    for send in sends:
        send.wait()
    whole = red2[0]
    for i in range(1, TORUS[0]):
        whole = whole + red2[i]
    count = 4 * math.prod(TORUS) * length
    mean = jnp.sum(whole, axis=1, keepdims=True) / count
    rms_ref[...] = jnp.broadcast_to(jnp.sqrt(mean + 1e-6), rms_ref.shape)


def body(data, spectra):
    vectors, own, length = data.shape
    freqs = length + 1
    sensors = spectra.shape[1]
    points = spectra.shape[2]
    forward, across, gains = spectral_tables(length)
    fh, fl = high_low(forward)
    ah, al = high_low(across)
    k_rows = jnp.transpose(
        spectra.reshape(2, sensors // LANES, LANES, points, freqs), (0, 4, 1, 3, 2)
    ).reshape(2, freqs * 8, LANES)
    steps = make_schedule()
    devices = math.prod(TORUS)
    vmem = pltpu.VMEM
    field, rms = pl.pallas_call(
        functools.partial(kernel, steps),
        out_shape=(
            jax.ShapeDtypeStruct((points * vectors, 512), F32),
            jax.ShapeDtypeStruct((vectors, LANES), F32),
        ),
        in_specs=[pl.BlockSpec(memory_space=pltpu.HBM)] * 7,
        out_specs=[pl.BlockSpec(memory_space=pltpu.VMEM)] * 2,
        scratch_shapes=[
            vmem((devices, ROWS, LANES), F32),
            vmem((vectors, own, length), F32),
            vmem((vectors * own, 512), F32),
            vmem((2, 4096, LANES), F32),
            vmem((4, sensors * 8, LANES), F32),
            vmem((512, 512), BF16),
            vmem((512, 512), BF16),
            vmem((2, 256, 256), BF16),
            vmem((2, 256, 256), BF16),
            vmem((8, 512), F32),
            vmem((192, LANES), F32),
            vmem((192, 512), F32),
            vmem((2, points * vectors, 512), F32),
            vmem((points * vectors, 512), F32),
            vmem((points * vectors, 512), F32),
            vmem((16, vectors, LANES), F32),
            vmem((8, vectors, LANES), F32),
            pltpu.SMEM((devices,), jnp.int32),
            pltpu.SemaphoreType.DMA((devices,)),
            pltpu.SemaphoreType.DMA((devices,)),
            pltpu.SemaphoreType.DMA((7,)),
            pltpu.SemaphoreType.DMA((2,)),
            pltpu.SemaphoreType.DMA((16,)),
            pltpu.SemaphoreType.DMA((16,)),
            pltpu.SemaphoreType.DMA((8,)),
            pltpu.SemaphoreType.DMA((8,)),
        ],
        compiler_params=pltpu.CompilerParams(
            collective_id=0, has_side_effects=True, vmem_limit_bytes=VMEM_LIMIT
        ),
        name="adjoint",
    )(data, k_rows, jnp.asarray(fh), jnp.asarray(fl), jnp.asarray(ah), jnp.asarray(al), jnp.asarray(gains, F32))
    scale = rms[:, 0]
    shaped = jnp.transpose(field.reshape(points, vectors, 512)[..., :length], (1, 0, 2))
    return (shaped / scale[:, None, None], scale)


def solution(mesh):
    split_mesh = Mesh(
        mesh.devices.reshape(*TORUS, mesh.shape["sensor"]), (*PARAM, "sensor")
    )
    placed = (P(None, SENSOR_PARAM, None), P(None, "sensor", PARAM, None))
    return jax.shard_map(
        body, mesh=split_mesh, in_specs=placed, out_specs=(P(None, PARAM, None), P()), check_vma=False
    )
```

time: 277 us -> 71.5 us (0.26)
  the two profiles are of different devices: /device:TPU:2 before, /device:TPU:1 now
where the time goes in v1:
time: 71.5 us; the launch traced here: 71.4 us
  Pallas kernels  68.2 us (95%)
  other arithmetic  1.67 us (2%)
  local copies, waits for them, and re-layouts  0.81 us (1%)
    pallas_call x1, Pallas kernels, body(): pl.pallas_call(functools.partial(kernel, steps), out_shape=(jax.ShapeDtyp...  68.2 us
    div x1, other arithmetic, body(): return (shaped / scale[:, None, None], scale)  1.67 us

profile of v1, /device:TPU:1, one launch (start us, length us, event | category | flops | bytes accessed | tf_op | source)
XLA Modules:
  0.0 71.4 jit_solution(11735935598511856762)
XLA Ops:
  0.6 68.2 %adjoint.1 = (f32[64,512]{1,0:T(8,128)}, f32[16,128]{1,0:T(8,128)}) custom-call(f32[16,2,420]{2,1,0:T(2,128)} %data_ref.1, f32[2,3368,128]{2,1,0:T(8,128)} %bitcast.9, bf16[512,512]{1,0:T(8,128)(2,1)} %constant.10.clone.fh_ref, bf16[512,512]{1,0:T(8,128)(2,1)} %constant.11.clone.fl_ref, bf16[2,256,256]{2,1,0:T(8,128)(2,1)} %constant.12.clone.ah_ref, ...), custom_call_target="tpu_custom_call" | custom-call | tf_op jit(solution)/shard_map/adjoint/pallas_call | solution.py:480
  68.9 0.8 %slice_reduce_fusion = f32[16]{0:T(128)S(1)} fusion(f32[16,128]{1,0:T(8,128)} %get-tuple-element.5), kind=kLoop, calls=%fused_computation.2 | loop fusion | bytes 128 | tf_op jit(solution)/shard_map/slice | solution.py:521
  69.7 0.0 copy-start
  69.7 1.7 %fusion = f32[16,4,420]{2,1,0:T(4,128)} fusion(f32[4,16,420]{2,1,0:T(8,128)} %bitcast.10, f32[16]{0:T(128)S(1)} %slice_reduce_fusion), kind=kLoop, calls=%fused_computation.1 | loop fusion | flops 26880 | bytes 215104 | tf_op jit(solution)/shard_map/div | solution.py:523
  71.4 0.0 copy-done
Async XLA Ops:
  69.7 1.7 %copy-start = (f32[16]{0:T(128)}, f32[16]{0:T(128)S(1)}, u32[]{:S(2)}) copy-start(f32[16]{0:T(128)S(1)} %slice_reduce_fusion) | copy-start | bytes 196

commit v2 on v1

--- a/solution.py
+++ b/solution.py
@@ -18,39 +18,43 @@
 BF16 = jnp.bfloat16
 TORUS = (8, 4, 4)
 DIRS = ((0, 1, 0), (0, -1, 0), (0, 0, 1), (0, 0, -1), (1, 0, 0), (-1, 0, 0))
-EXTRA = (2, 0, 0)
+EXTRA = (1, 1, 0)
 ROWS = 112
+SENT = 107
+LAG = 4
+SEED = 80
 LANES = 128
 PIECE = 45
 REST = 37
-SETUP_STEPS = 4
-VMEM_LIMIT = 66_800_000
+UNROLL = 6
+VMEM_LIMIT = 66_000_000
 
 
 def moved(offset, step):
     return tuple((a + b) % n for a, b, n in zip(offset, step, TORUS))
 
 
-def attempt(seed):
-    rng = random.Random(seed)
+def make_schedule():
+    rng = random.Random(SEED)
     got = {(0, 0, 0): 0, EXTRA: 2}
     steps = []
-    number = (math.prod(TORUS) - 2) // 6
+    number = (math.prod(TORUS) - 2) // len(DIRS)
     for k in range(1, number + 1):
-        for lag in (3, 2, 1):
+        for lag in range(LAG, 0, -1):
             cand = []
-            for d in range(6):
+            for d in range(len(DIRS)):
                 edges = []
                 for p, s in got.items():
                     c = moved(p, DIRS[d])
                     if c in got or (s > 0 and s > k - min(lag, max(1, k - 1))):
                         continue
-                    edges.append((s, rng.random(), p, c))
+                    key = 0 if k <= LAG else -sum(moved(c, e) not in got for e in DIRS)
+                    edges.append((key, rng.random(), p, c))
                 cand.append(sorted(edges))
             used = {}
 
             def augment(d, seen):
-                for s, _, p, c in cand[d]:
+                for _, _, p, c in cand[d]:
                     if c in seen:
                         continue
                     seen.add(c)
@@ -59,25 +63,14 @@
                         return True
                 return False
 
-            count = sum(augment(d, set()) for d in sorted(range(6), key=lambda d: len(cand[d])))
-            if count == 6:
+            order = sorted(range(len(DIRS)), key=lambda d: len(cand[d]))
+            if sum(augment(d, set()) for d in order) == len(DIRS):
                 break
-        else:
-            return None
         for c, (d, p) in used.items():
             got[c] = k
         steps.append(sorted((d, p, c) for c, (d, p) in used.items()))
-    lags = [k - got[p] for k, step in enumerate(steps, 1) for d, p, c in step if got[p] > 0 and k > 3]
-    return (sum(10 ** (3 - lag) for lag in lags if lag < 3), steps)
-
-
-def make_schedule():
-    best = None
-    for seed in range(150):
-        found = attempt(seed)
-        if found and (best is None or found[0] < best[0]):
-            best = found
-    return best[1]
+    assert len(got) == math.prod(TORUS)
+    return steps
 
 
 def spectral_tables(steps):
@@ -161,10 +154,7 @@
     recv_sem,
     load_sem,
     pair_sem,
-    r1_send,
-    r1_recv,
-    r2_send,
-    r2_recv,
+    red_sem,
 ):
     vectors, own, length = data_ref.shape
     me = tuple(lax.axis_index(name) for name in PARAM)
@@ -175,6 +165,7 @@
             name: lax.rem(pos + (o % n), n) for name, pos, o, n in zip(PARAM, me, offset, TORUS)
         }
 
+    beside = [device(offset) for offset in DIRS]
     partner = {"sensor": 1 - core}
     barrier = pltpu.get_barrier_semaphore()
     for offset in DIRS + (tuple(-o for o in EXTRA),):
@@ -206,19 +197,31 @@
         for d, p, c in step:
             pending.setdefault(step_of[p], []).append((d, p, c))
 
-    def copy(source, target, offset):
+    def copy(source, target, count, step, where):
         return pltpu.make_async_remote_copy(
-            src_ref=gat.at[source],
-            dst_ref=gat.at[target],
-            send_sem=send_sem.at[target],
-            recv_sem=recv_sem.at[target],
-            device_id=device(offset),
+            src_ref=gat.at[pl.ds(source, count), pl.ds(0, SENT)],
+            dst_ref=gat.at[pl.ds(target, count), pl.ds(0, SENT)],
+            send_sem=send_sem,
+            recv_sem=recv_sem.at[step],
+            device_id=where,
             device_id_type=MESH,
         )
 
     def forward_after(k):
         for d, p, c in pending.get(k, ()):
-            copy(slot_of[p], slot_of[c], DIRS[d]).start()
+            target = slot_of[c]
+            copy(slot_of[p], target, 1, (target + 4) // 6, beside[d]).start()
+
+    def forward_between(k, low, high):
+        if high - low == 1:
+            forward_after(low)
+        else:
+            middle = (low + high) // 2
+            lax.cond(
+                k < middle,
+                lambda: forward_between(k, low, middle),
+                lambda: forward_between(k, middle, high),
+            )
 
     xs[:, pl.ds(384, LANES)] = jnp.zeros((2 * vectors, LANES), F32)
     loads[0].wait()
@@ -242,11 +245,16 @@
         pltpu.roll(rest[8 * g : 8 * g + 8], (REST * (g % 3) - PIECE) % LANES, 1) for g in range(4)
     ]
     gat[0, pl.ds(96, 8), :] = groups[0] + groups[1] + groups[2]
-    gat[0, pl.ds(104, 8), :] = groups[3]
+    row8 = lax.broadcasted_iota(jnp.int32, (8, LANES), 0)
+    folded = jnp.where(row8 < 3, groups[3], 0.0)
+    for i in (1, 2):
+        third = jnp.where((row8 >= 3 * i) & (row8 < 3 * i + 3), groups[3], 0.0)
+        folded = folded + pltpu.roll(pltpu.roll(third, 8 - 3 * i, 0), REST * i, 1)
+    gat[0, pl.ds(104, 8), :] = folded
 
     pl.semaphore_wait(barrier, 8)
     forward_after(0)
-    copy(0, 1, EXTRA).start()
+    copy(0, 1, 1, 0, device(EXTRA)).start()
 
     for offset, slot in slot_of.items():
         z, x, y = (
@@ -279,8 +287,6 @@
                     turned = jnp.where(first, 0.0, turned)
                 kt[ft, pl.ds(st * LANES * 8 + c * 4 + p, LANES, stride=8), :] = turned
 
-    def wait_slot(slot):
-        copy(0, slot, DIRS[0]).wait_recv()
 
     def consume(first, count):
         number = 32 * count
@@ -289,8 +295,17 @@
             left = gat[first + j, pl.ds(96, 16), :]
             moved2 = pltpu.roll(tile2, PIECE, 1)
             for g in range(4):
-                source = left[8:16] if g == 3 else left[0:8]
-                back = pltpu.roll(source, (PIECE - REST * (g % 3)) % LANES, 1)
+                if g < 3:
+                    back = pltpu.roll(left[0:8], (PIECE - REST * g) % LANES, 1)
+                else:
+                    thirds = [
+                        pltpu.roll(left[8:16], (PIECE - REST * i) % LANES, 1) for i in range(3)
+                    ]
+                    back = jnp.where(
+                        row8 < 3,
+                        thirds[0],
+                        jnp.where(row8 < 6, pltpu.roll(thirds[1], 3, 0), pltpu.roll(thirds[2], 6, 0)),
+                    )
                 value = jnp.where(
                     lane8 < PIECE,
                     moved2[8 * g : 8 * g + 8],
@@ -343,44 +358,37 @@
                             sums[8 + i] = sums[8 + i] + k_re * d_im[h] - k_im * d_re[h]
                 return tuple(sums)
 
-            final = lax.fori_loop(0, count, sensors, start)
+            final = lax.fori_loop(0, count, sensors, start, unroll=UNROLL if count % UNROLL == 0 else 1)
             for i, value in enumerate(final):
                 c, p, h = i // 8, i // 2 % 4, i % 2
                 acc[c, pl.ds(p * 16 + h * 8, 8), pl.ds(ft * LANES, LANES)] = value
 
+    for ft in range(3):
+        transpose_tile(ft)
     last = len(steps)
 
     @pl.loop(1, last + 1)
     def _(k):
-        for i in range(6):
-            wait_slot(2 + 6 * (k - 1) + i)
+        copy(0, 6 * k - 4, 6, k, beside[0]).wait_recv()
 
         @pl.when(k == 2)
         def _():
-            wait_slot(1)
-
-        for number in range(1, last):
-            if number in pending:
-
-                @pl.when(k == number)
-                def _():
-                    forward_after(number)
-
-        @pl.when(k <= SETUP_STEPS)
+            copy(0, 1, 1, 0, beside[0]).wait_recv()
+
+        @pl.when(k < last)
         def _():
-            for ft in range(4):
-
-                @pl.when(k == ft + 1)
-                def _():
-                    transpose_tile(ft)
-
-        @pl.when(k == SETUP_STEPS)
+            forward_between(k, 1, last)
+
+        @pl.when(k == 1)
+        def _():
+            transpose_tile(3)
+
+        @pl.when(k == 2)
         def _():
             consume(0, 2)
 
-        caught = 2 * SETUP_STEPS
-        low = jnp.where(k <= SETUP_STEPS, 0, jnp.where(k <= caught, 2 * (k - SETUP_STEPS) - 2, k - 1))
-        high = jnp.where(k <= SETUP_STEPS, 0, jnp.where(k <= caught, 2 * (k - SETUP_STEPS), k))
+        low = jnp.where(k == 2, 0, k - 1)
+        high = jnp.where(k == 1, 0, k)
 
         @pl.loop(low, high)
         def _(b):
@@ -403,64 +411,58 @@
         device_id_type=MESH,
     )
     swap.start()
-    for slot in range(1, gat.shape[0]):
-        copy(0, slot, DIRS[0]).wait_send()
+    copy(1, 1, gat.shape[0] - 1, 0, beside[0]).wait_send()
     swap.wait()
     field = part[...] + other[...]
-    field_ref[...] = field
     square = field * field
     square = square[:, 0:128] + square[:, 128:256] + square[:, 256:384] + square[:, 384:512]
     square = square[0:16] + square[16:32] + square[32:48] + square[48:64]
-
+    diagonal = lax.broadcasted_iota(jnp.int32, (16, LANES), 0) == lax.broadcasted_iota(
+        jnp.int32, (16, LANES), 1
+    )
+    column = jnp.sum(square, axis=1, keepdims=True)
     z, x, y = me
     spot = x * TORUS[2] + y
-    red1[spot] = square
-    sends = []
-    for dx in range(TORUS[1]):
-        for dy in range(TORUS[2]):
-            i = dx * TORUS[2] + dy
-            if i == 0:
-                continue
-            sends.append(
-                pltpu.make_async_remote_copy(
-                    src_ref=red1.at[spot],
-                    dst_ref=red1.at[spot],
-                    send_sem=r1_send.at[i],
-                    recv_sem=r1_recv.at[i],
-                    device_id=device((0, dx, dy)),
-                    device_id_type=MESH,
-                )
-            )
-    for send in sends:
-        send.start()
-    for send in sends:
-        send.wait()
-    plane = red1[0]
-    for i in range(1, TORUS[1] * TORUS[2]):
-        plane = plane + red1[i]
-    red2[z] = plane
-    sends = []
-    for dz in range(1, TORUS[0]):
-        sends.append(
+    red1[spot] = jnp.sum(jnp.where(diagonal, column, 0.0), axis=0, keepdims=True)
+
+    def spread(ref, mine, first, offsets):
+        sends = [
             pltpu.make_async_remote_copy(
-                src_ref=red2.at[z],
-                dst_ref=red2.at[z],
-                send_sem=r2_send.at[dz],
-                recv_sem=r2_recv.at[dz],
-                device_id=device((dz, 0, 0)),
+                src_ref=ref.at[pl.ds(mine, 1)],
+                dst_ref=ref.at[pl.ds(mine, 1)],
+                send_sem=red_sem.at[first],
+                recv_sem=red_sem.at[first + 1],
+                device_id=device(offset),
                 device_id_type=MESH,
             )
+            for offset in offsets
+        ]
+        for send in sends:
+            send.start()
+        every = ref.at[pl.ds(0, len(offsets))]
+        whole = pltpu.make_async_remote_copy(
+            src_ref=every,
+            dst_ref=every,
+            send_sem=red_sem.at[first],
+            recv_sem=red_sem.at[first + 1],
+            device_id=beside[0],
+            device_id_type=MESH,
         )
-    for send in sends:
-        send.start()
-    for send in sends:
-        send.wait()
-    whole = red2[0]
-    for i in range(1, TORUS[0]):
-        whole = whole + red2[i]
+        whole.wait()
+        total = ref[0]
+        for i in range(1, len(offsets) + 1):
+            total = total + ref[i]
+        return total
+
+    plane = [(0, dx, dy) for dx in range(TORUS[1]) for dy in range(TORUS[2]) if dx + dy > 0]
+    red2[z] = spread(red1, spot, 0, plane)
+    whole = spread(red2, z, 2, [(dz, 0, 0) for dz in range(1, TORUS[0])])
     count = 4 * math.prod(TORUS) * length
-    mean = jnp.sum(whole, axis=1, keepdims=True) / count
-    rms_ref[...] = jnp.broadcast_to(jnp.sqrt(mean + 1e-6), rms_ref.shape)
+    rms = jnp.sqrt(whole / count + 1e-6)
+    rms_ref[...] = rms
+    column = jnp.sum(jnp.where(diagonal, 1.0 / rms, 0.0), axis=1, keepdims=True)
+    for p in range(4):
+        field_ref[:, p, :] = field[16 * p : 16 * p + 16, 0:length] * column
 
 
 def body(data, spectra):
@@ -480,8 +482,8 @@
     field, rms = pl.pallas_call(
         functools.partial(kernel, steps),
         out_shape=(
-            jax.ShapeDtypeStruct((points * vectors, 512), F32),
-            jax.ShapeDtypeStruct((vectors, LANES), F32),
+            pltpu.VMEM((vectors, points, length), F32),
+            pltpu.VMEM((1, LANES), F32),
         ),
         in_specs=[pl.BlockSpec(memory_space=pltpu.HBM)] * 7,
         out_specs=[pl.BlockSpec(memory_space=pltpu.VMEM)] * 2,
@@ -501,26 +503,21 @@
             vmem((2, points * vectors, 512), F32),
             vmem((points * vectors, 512), F32),
             vmem((points * vectors, 512), F32),
-            vmem((16, vectors, LANES), F32),
-            vmem((8, vectors, LANES), F32),
+            vmem((16, 1, LANES), F32),
+            vmem((8, 1, LANES), F32),
             pltpu.SMEM((devices,), jnp.int32),
-            pltpu.SemaphoreType.DMA((devices,)),
-            pltpu.SemaphoreType.DMA((devices,)),
+            pltpu.SemaphoreType.DMA,
+            pltpu.SemaphoreType.DMA((len(steps) + 1,)),
             pltpu.SemaphoreType.DMA((7,)),
             pltpu.SemaphoreType.DMA((2,)),
-            pltpu.SemaphoreType.DMA((16,)),
-            pltpu.SemaphoreType.DMA((16,)),
-            pltpu.SemaphoreType.DMA((8,)),
-            pltpu.SemaphoreType.DMA((8,)),
+            pltpu.SemaphoreType.DMA((4,)),
         ],
         compiler_params=pltpu.CompilerParams(
             collective_id=0, has_side_effects=True, vmem_limit_bytes=VMEM_LIMIT
         ),
         name="adjoint",
     )(data, k_rows, jnp.asarray(fh), jnp.asarray(fl), jnp.asarray(ah), jnp.asarray(al), jnp.asarray(gains, F32))
-    scale = rms[:, 0]
-    shaped = jnp.transpose(field.reshape(points, vectors, 512)[..., :length], (1, 0, 2))
-    return (shaped / scale[:, None, None], scale)
+    return (field, rms[0, :vectors])
 
 
 def solution(mesh):

time: 71.5 us -> 57.7 us (0.81)
  Pallas kernels: 68.2 us -> 55.9 us
  other arithmetic: 1.67 us -> 0 us
    pallas_call x1, Pallas kernels: 68.2 us -> 55.9 us  [body(): pl.pallas_call(functools.partial(kernel, steps), out_shape=(pltpu.VMEM((v...]
    div x1 -> x0, other arithmetic: 1.67 us -> none  [body(): return (shaped / scale[:, None, None], scale)]
    slice x1 -> x0, local copies, waits for them, and re-layouts: 0.81 us -> none  [body(): scale = rms[:, 0]]
where the time goes in v2:
time: 57.7 us
  Pallas kernels  55.9 us (97%)
  local copies, waits for them, and re-layouts  1.17 us (2%)
  between operations  0.64 us (1%)
    pallas_call x1, Pallas kernels, body(): pl.pallas_call(functools.partial(kernel, steps), out_shape=(pltpu.VMEM((v...  55.9 us

profile of v2, /device:TPU:1, one launch (start us, length us, event | category | flops | bytes accessed | tf_op | source)
XLA Modules:
  0.0 57.7 jit_solution(16227314197721691460)
XLA Ops:
  0.6 55.9 %adjoint.1 = (f32[16,4,420]{2,1,0:T(4,128)S(1)}, f32[1,128]{1,0:T(1,128)S(1)}) custom-call(f32[16,2,420]{2,1,0:T(2,128)} %data_ref.1, f32[2,3368,128]{2,1,0:T(8,128)} %bitcast.7, bf16[512,512]{1,0:T(8,128)(2,1)} %constant.10.clone.fh_ref, bf16[512,512]{1,0:T(8,128)(2,1)} %constant.11.clone.fl_ref, bf16[2,256,256]{2,1,0:T(8,128)(2,1)} %constant.12.clone.ah_ref, ...), custom_call_target="tpu_custom_call" | custom-call | tf_op jit(solution)/shard_map/adjoint/pallas_call | solution.py:482
  56.5 0.7 %copy.11 = f32[16,4,420]{2,1,0:T(4,128)} copy(f32[16,4,420]{2,1,0:T(4,128)S(1)} %get-tuple-element.6) | data formatting | bytes 215040
  57.2 0.5 slice_bitcast_fusion

commit v3 on v2

--- a/solution.py
+++ b/solution.py
@@ -1,6 +1,5 @@
 import functools
 import math
-import random
 
 import jax
 import jax.numpy as jnp
@@ -17,60 +16,56 @@
 F32 = jnp.float32
 BF16 = jnp.bfloat16
 TORUS = (8, 4, 4)
-DIRS = ((0, 1, 0), (0, -1, 0), (0, 0, 1), (0, 0, -1), (1, 0, 0), (-1, 0, 0))
-EXTRA = (1, 1, 0)
+VECTORS = (
+    (0, 1, 0),
+    (0, -1, 0),
+    (0, 0, 1),
+    (0, 0, -1),
+    (1, 0, 0),
+    (-1, 0, 0),
+    (-1, 0, 1),
+    (0, -1, -1),
+    (1, 1, 0),
+)
+COPIES = (
+    (0, 0, 0, 3), (0, 0, 1, 4), (0, 0, 2, 1), (0, 0, 3, 2), (0, 0, 4, 5),
+    (0, 0, 5, 6), (1, 2, 0, 8), (1, 6, 1, 12), (1, 5, 2, 9), (1, 2, 3, 7),
+    (1, 6, 5, 11), (1, 5, 4, 10), (1, 6, 3, 17), (1, 3, 5, 18), (1, 4, 4, 16),
+    (1, 3, 2, 13), (1, 4, 1, 14), (1, 5, 0, 15), (1, 2, 1, 20), (1, 5, 3, 21),
+    (1, 4, 2, 19), (1, 1, 5, 22), (2, 8, 8, 23), (2, 11, 6, 24), (2, 12, 7, 25),
+    (2, 10, 4, 28), (2, 11, 3, 30), (2, 11, 5, 29), (2, 11, 0, 31), (2, 10, 1, 27),
+    (2, 10, 2, 26), (2, 12, 5, 37), (2, 10, 0, 35), (2, 11, 2, 36), (2, 7, 1, 32),
+    (2, 10, 3, 34), (2, 7, 4, 33), (3, 8, 3, 38), (3, 18, 2, 43), (3, 9, 0, 39),
+    (3, 7, 5, 42), (3, 9, 1, 41), (3, 8, 4, 40), (4, 24, 2, 47), (4, 24, 0, 48),
+    (4, 24, 5, 46), (4, 23, 4, 45), (4, 24, 1, 49), (4, 23, 3, 44), (4, 13, 0, 50),
+    (4, 22, 1, 54), (4, 8, 5, 53), (4, 12, 3, 55), (4, 14, 4, 51), (4, 23, 0, 57),
+    (4, 14, 3, 56), (4, 14, 5, 61), (5, 27, 2, 52), (5, 27, 4, 59), (5, 26, 2, 58),
+    (5, 30, 1, 60), (6, 25, 3, 67), (6, 28, 2, 63), (6, 29, 1, 65), (6, 35, 4, 64),
+    (6, 26, 0, 62), (6, 25, 5, 66), (7, 29, 0, 72), (7, 28, 3, 69), (7, 31, 2, 73),
+    (7, 28, 4, 70), (7, 34, 1, 68), (7, 30, 5, 71), (8, 45, 4, 75), (8, 48, 0, 79),
+    (8, 46, 2, 76), (8, 46, 1, 78), (8, 48, 5, 77), (8, 45, 3, 74), (9, 47, 0, 83),
+    (9, 52, 4, 82), (9, 49, 2, 84), (9, 54, 5, 85), (9, 35, 3, 80), (9, 52, 1, 81),
+    (10, 42, 5, 90), (10, 59, 1, 88), (10, 31, 3, 91), (10, 58, 0, 86), (10, 59, 4, 89),
+    (10, 52, 2, 87), (11, 63, 0, 92), (11, 66, 2, 96), (11, 66, 3, 97), (11, 65, 1, 94),
+    (11, 64, 4, 93), (11, 66, 5, 95), (12, 68, 4, 100), (12, 54, 1, 103), (12, 63, 2, 98),
+    (12, 71, 5, 101), (12, 64, 3, 99), (12, 42, 0, 102), (13, 75, 3, 104), (13, 77, 0, 106),
+    (13, 77, 2, 105), (13, 75, 4, 107), (13, 76, 1, 108), (13, 60, 5, 109), (14, 84, 4, 114),
+    (14, 72, 3, 111), (14, 79, 2, 112), (14, 32, 5, 115), (14, 73, 0, 113), (14, 32, 1, 110),
+    (15, 89, 3, 121), (15, 88, 2, 118), (15, 33, 0, 116), (15, 87, 4, 119), (15, 87, 5, 117),
+    (15, 89, 1, 120), (16, 83, 4, 126), (16, 81, 5, 122), (16, 92, 2, 124), (16, 35, 0, 123),
+    (16, 93, 3, 125), (18, 108, 1, 127),
+)
 ROWS = 112
 SENT = 107
-LAG = 4
-SEED = 80
+GROUP = 6
 LANES = 128
 PIECE = 45
 REST = 37
-UNROLL = 6
 VMEM_LIMIT = 66_000_000
 
 
 def moved(offset, step):
     return tuple((a + b) % n for a, b, n in zip(offset, step, TORUS))
-
-
-def make_schedule():
-    rng = random.Random(SEED)
-    got = {(0, 0, 0): 0, EXTRA: 2}
-    steps = []
-    number = (math.prod(TORUS) - 2) // len(DIRS)
-    for k in range(1, number + 1):
-        for lag in range(LAG, 0, -1):
-            cand = []
-            for d in range(len(DIRS)):
-                edges = []
-                for p, s in got.items():
-                    c = moved(p, DIRS[d])
-                    if c in got or (s > 0 and s > k - min(lag, max(1, k - 1))):
-                        continue
-                    key = 0 if k <= LAG else -sum(moved(c, e) not in got for e in DIRS)
-                    edges.append((key, rng.random(), p, c))
-                cand.append(sorted(edges))
-            used = {}
-
-            def augment(d, seen):
-                for _, _, p, c in cand[d]:
-                    if c in seen:
-                        continue
-                    seen.add(c)
-                    if c not in used or augment(used[c][0], seen):
-                        used[c] = (d, p)
-                        return True
-                return False
-
-            order = sorted(range(len(DIRS)), key=lambda d: len(cand[d]))
-            if sum(augment(d, set()) for d in order) == len(DIRS):
-                break
-        for c, (d, p) in used.items():
-            got[c] = k
-        steps.append(sorted((d, p, c) for c, (d, p) in used.items()))
-    assert len(got) == math.prod(TORUS)
-    return steps
 
 
 def spectral_tables(steps):
@@ -122,7 +117,6 @@
 
 
 def kernel(
-    steps,
     data_ref,
     k_ref,
     fh_ref,
@@ -165,11 +159,11 @@
             name: lax.rem(pos + (o % n), n) for name, pos, o, n in zip(PARAM, me, offset, TORUS)
         }
 
-    beside = [device(offset) for offset in DIRS]
+    beside = [device(offset) for offset in VECTORS]
     partner = {"sensor": 1 - core}
     barrier = pltpu.get_barrier_semaphore()
-    for offset in DIRS + (tuple(-o for o in EXTRA),):
-        pl.semaphore_signal(barrier, inc=1, device_id=device(offset), device_id_type=MESH)
+    for where in beside[:6]:
+        pl.semaphore_signal(barrier, inc=1, device_id=where, device_id_type=MESH)
     pl.semaphore_signal(barrier, inc=1, device_id=partner, device_id_type=MESH)
 
     rows_k = k_ref.shape[1]
@@ -185,17 +179,11 @@
     for load in loads:
         load.start()
 
-    slot_of = {(0, 0, 0): 0, EXTRA: 1}
-    for k, step in enumerate(steps):
-        for i, (d, p, c) in enumerate(step):
-            slot_of[c] = 2 + 6 * k + i
-    step_of = {c: k for k, step in enumerate(steps, 1) for d, p, c in step}
-    step_of[(0, 0, 0)] = 0
-    step_of[EXTRA] = 2
-    pending = {}
-    for k, step in enumerate(steps):
-        for d, p, c in step:
-            pending.setdefault(step_of[p], []).append((d, p, c))
+    offsets = {0: (0, 0, 0)}
+    for _, source, vector, target in COPIES:
+        offsets[target] = moved(offsets[source], VECTORS[vector])
+    last = (len(COPIES) - 1) // GROUP + 1
+    rest_of = len(COPIES) - GROUP * (last - 1)
 
     def copy(source, target, count, step, where):
         return pltpu.make_async_remote_copy(
@@ -208,9 +196,9 @@
         )
 
     def forward_after(k):
-        for d, p, c in pending.get(k, ()):
-            target = slot_of[c]
-            copy(slot_of[p], target, 1, (target + 4) // 6, beside[d]).start()
+        for when, source, vector, target in COPIES:
+            if when == k:
+                copy(source, target, 1, (target - 1) // GROUP, beside[vector]).start()
 
     def forward_between(k, low, high):
         if high - low == 1:
@@ -252,11 +240,9 @@
         folded = folded + pltpu.roll(pltpu.roll(third, 8 - 3 * i, 0), REST * i, 1)
     gat[0, pl.ds(104, 8), :] = folded
 
-    pl.semaphore_wait(barrier, 8)
+    pl.semaphore_wait(barrier, 7)
     forward_after(0)
-    copy(0, 1, 1, 0, device(EXTRA)).start()
-
-    for offset, slot in slot_of.items():
+    for slot, offset in offsets.items():
         z, x, y = (
             lax.rem(pos + n - o, n) for pos, o, n in zip(me, offset, TORUS)
         )
@@ -358,26 +344,18 @@
                             sums[8 + i] = sums[8 + i] + k_re * d_im[h] - k_im * d_re[h]
                 return tuple(sums)
 
-            final = lax.fori_loop(0, count, sensors, start, unroll=UNROLL if count % UNROLL == 0 else 1)
+            final = lax.fori_loop(0, count, sensors, start, unroll=True)
             for i, value in enumerate(final):
                 c, p, h = i // 8, i // 2 % 4, i % 2
                 acc[c, pl.ds(p * 16 + h * 8, 8), pl.ds(ft * LANES, LANES)] = value
 
     for ft in range(3):
         transpose_tile(ft)
-    last = len(steps)
-
-    @pl.loop(1, last + 1)
+
+    @pl.loop(1, last)
     def _(k):
-        copy(0, 6 * k - 4, 6, k, beside[0]).wait_recv()
-
-        @pl.when(k == 2)
-        def _():
-            copy(0, 1, 1, 0, beside[0]).wait_recv()
-
-        @pl.when(k < last)
-        def _():
-            forward_between(k, 1, last)
+        copy(0, GROUP * k - 5, GROUP, k - 1, beside[0]).wait_recv()
+        forward_between(k, 1, last)
 
         @pl.when(k == 1)
         def _():
@@ -385,14 +363,17 @@
 
         @pl.when(k == 2)
         def _():
-            consume(0, 2)
+            consume(0, 1)
 
         low = jnp.where(k == 2, 0, k - 1)
         high = jnp.where(k == 1, 0, k)
 
         @pl.loop(low, high)
         def _(b):
-            consume(2 + 6 * b, 6)
+            consume(1 + GROUP * b, GROUP)
+
+    copy(0, GROUP * (last - 1) + 1, rest_of, last - 1, beside[0]).wait_recv()
+    consume(GROUP * (last - 1) + 1, rest_of)
 
     out_re = acc[0] * gain[0:1, :]
     out_im = acc[1] * gain[1:2, :]
@@ -420,46 +401,51 @@
     diagonal = lax.broadcasted_iota(jnp.int32, (16, LANES), 0) == lax.broadcasted_iota(
         jnp.int32, (16, LANES), 1
     )
-    column = jnp.sum(square, axis=1, keepdims=True)
     z, x, y = me
     spot = x * TORUS[2] + y
-    red1[spot] = jnp.sum(jnp.where(diagonal, column, 0.0), axis=0, keepdims=True)
-
-    def spread(ref, mine, first, offsets):
-        sends = [
-            pltpu.make_async_remote_copy(
-                src_ref=ref.at[pl.ds(mine, 1)],
-                dst_ref=ref.at[pl.ds(mine, 1)],
-                send_sem=red_sem.at[first],
-                recv_sem=red_sem.at[first + 1],
-                device_id=device(offset),
-                device_id_type=MESH,
-            )
-            for offset in offsets
-        ]
-        for send in sends:
-            send.start()
-        every = ref.at[pl.ds(0, len(offsets))]
-        whole = pltpu.make_async_remote_copy(
-            src_ref=every,
-            dst_ref=every,
+
+    def message(ref, mine, count, first, where):
+        part_of = ref.at[pl.ds(mine, count)]
+        return pltpu.make_async_remote_copy(
+            src_ref=part_of,
+            dst_ref=part_of,
             send_sem=red_sem.at[first],
             recv_sem=red_sem.at[first + 1],
-            device_id=beside[0],
+            device_id=where,
             device_id_type=MESH,
         )
-        whole.wait()
+
+    def total_of(ref):
         total = ref[0]
-        for i in range(1, len(offsets) + 1):
+        for i in range(1, ref.shape[0]):
             total = total + ref[i]
         return total
 
-    plane = [(0, dx, dy) for dx in range(TORUS[1]) for dy in range(TORUS[2]) if dx + dy > 0]
-    red2[z] = spread(red1, spot, 0, plane)
-    whole = spread(red2, z, 2, [(dz, 0, 0) for dz in range(1, TORUS[0])])
+    @pl.when(core == 1)
+    def _():
+        column = jnp.sum(square, axis=1, keepdims=True)
+        red1[spot] = jnp.sum(jnp.where(diagonal, column, 0.0), axis=0, keepdims=True)
+        peers = [(0, dx, dy) for dx in range(TORUS[1]) for dy in range(TORUS[2]) if dx + dy > 0]
+        for offset in peers:
+            message(red1, spot, 1, 0, device(offset)).start()
+        message(red1, 0, len(peers), 0, beside[0]).wait()
+        red2[z] = total_of(red1)
+        line = [(dz, 0, 0) for dz in range(TORUS[0])]
+        for offset in line[1:]:
+            message(red2, z, 1, 2, device(offset)).start()
+        for offset in line:
+            message(red2, z, 1, 2, dict(device(offset), sensor=0)).start()
+        message(red2, 0, TORUS[0] - 1, 2, beside[0]).wait_recv()
+        message(red1, 0, 2 * TORUS[0] - 1, 2, beside[0]).wait_send()
+
+    @pl.when(core == 0)
+    def _():
+        message(red2, 0, TORUS[0], 2, beside[0]).wait_recv()
+
+    whole = total_of(red2)
     count = 4 * math.prod(TORUS) * length
     rms = jnp.sqrt(whole / count + 1e-6)
-    rms_ref[...] = rms
+    rms_ref[...] = rms[0, 0:16]
     column = jnp.sum(jnp.where(diagonal, 1.0 / rms, 0.0), axis=1, keepdims=True)
     for p in range(4):
         field_ref[:, p, :] = field[16 * p : 16 * p + 16, 0:length] * column
@@ -476,14 +462,13 @@
     k_rows = jnp.transpose(
         spectra.reshape(2, sensors // LANES, LANES, points, freqs), (0, 4, 1, 3, 2)
     ).reshape(2, freqs * 8, LANES)
-    steps = make_schedule()
     devices = math.prod(TORUS)
     vmem = pltpu.VMEM
     field, rms = pl.pallas_call(
-        functools.partial(kernel, steps),
+        kernel,
         out_shape=(
             pltpu.VMEM((vectors, points, length), F32),
-            pltpu.VMEM((1, LANES), F32),
+            pltpu.VMEM((vectors,), F32),
         ),
         in_specs=[pl.BlockSpec(memory_space=pltpu.HBM)] * 7,
         out_specs=[pl.BlockSpec(memory_space=pltpu.VMEM)] * 2,
@@ -507,7 +492,7 @@
             vmem((8, 1, LANES), F32),
             pltpu.SMEM((devices,), jnp.int32),
             pltpu.SemaphoreType.DMA,
-            pltpu.SemaphoreType.DMA((len(steps) + 1,)),
+            pltpu.SemaphoreType.DMA(((len(COPIES) - 1) // GROUP + 1,)),
             pltpu.SemaphoreType.DMA((7,)),
             pltpu.SemaphoreType.DMA((2,)),
             pltpu.SemaphoreType.DMA((4,)),
@@ -517,7 +502,7 @@
         ),
         name="adjoint",
     )(data, k_rows, jnp.asarray(fh), jnp.asarray(fl), jnp.asarray(ah), jnp.asarray(al), jnp.asarray(gains, F32))
-    return (field, rms[0, :vectors])
+    return (field, rms)
 
 
 def solution(mesh):

time: 57.7 us -> 54.2 us (0.939)
  Pallas kernels: 55.9 us -> 52.3 us
    pallas_call x1, Pallas kernels: 55.9 us -> 52.3 us  [body(): pl.pallas_call(kernel, out_shape=(pltpu.VMEM((vectors, points, length), F...]
    unnamed x1 -> x2, local copies, waits for them, and re-layouts: 0.66 us -> 1.17 us
where the time goes in v3:
time: 54.2 us; the launch traced here: 54.1 us
  Pallas kernels  52.3 us (96%)
  local copies, waits for them, and re-layouts  1.17 us (2%)
  between operations  0.64 us (1%)
    pallas_call x1, Pallas kernels, body(): pl.pallas_call(kernel, out_shape=(pltpu.VMEM((vectors, points, length), F...  52.3 us
    unnamed x2, local copies, waits for them, and re-layouts  1.17 us

profile of v3, /device:TPU:1, one launch (start us, length us, event | category | flops | bytes accessed | tf_op | source)
XLA Modules:
  0.0 54.1 jit_solution(9501710207911524798)
XLA Ops:
  0.6 52.3 %adjoint.1 = (f32[16,4,420]{2,1,0:T(4,128)S(1)}, f32[16]{0:T(128)S(1)}) custom-call(f32[16,2,420]{2,1,0:T(2,128)} %data_ref.1, f32[2,3368,128]{2,1,0:T(8,128)} %bitcast.5, bf16[512,512]{1,0:T(8,128)(2,1)} %constant.10.clone.fh_ref, bf16[512,512]{1,0:T(8,128)(2,1)} %constant.11.clone.fl_ref, bf16[2,256,256]{2,1,0:T(8,128)(2,1)} %constant.12.clone.ah_ref, ...), custom_call_target="tpu_custom_call" | custom-call | tf_op jit(solution)/shard_map/adjoint/pallas_call | solution.py:467
  52.9 0.7 %copy.12 = f32[16,4,420]{2,1,0:T(4,128)} copy(f32[16,4,420]{2,1,0:T(4,128)S(1)} %get-tuple-element.2) | data formatting | bytes 215040
  53.6 0.5 copy.13

commit v4 on v3

--- a/solution.py
+++ b/solution.py
@@ -23,37 +23,42 @@
     (0, 0, -1),
     (1, 0, 0),
     (-1, 0, 0),
-    (-1, 0, 1),
+    (-1, -1, 0),
+    (-1, 0, -1),
     (0, -1, -1),
-    (1, 1, 0),
+    (0, 1, -1),
+    (0, 1, 1),
+    (1, -1, 0),
+    (1, 0, 1),
+    (2, 0, 0),
 )
 COPIES = (
     (0, 0, 0, 3), (0, 0, 1, 4), (0, 0, 2, 1), (0, 0, 3, 2), (0, 0, 4, 5),
-    (0, 0, 5, 6), (1, 2, 0, 8), (1, 6, 1, 12), (1, 5, 2, 9), (1, 2, 3, 7),
-    (1, 6, 5, 11), (1, 5, 4, 10), (1, 6, 3, 17), (1, 3, 5, 18), (1, 4, 4, 16),
-    (1, 3, 2, 13), (1, 4, 1, 14), (1, 5, 0, 15), (1, 2, 1, 20), (1, 5, 3, 21),
-    (1, 4, 2, 19), (1, 1, 5, 22), (2, 8, 8, 23), (2, 11, 6, 24), (2, 12, 7, 25),
-    (2, 10, 4, 28), (2, 11, 3, 30), (2, 11, 5, 29), (2, 11, 0, 31), (2, 10, 1, 27),
-    (2, 10, 2, 26), (2, 12, 5, 37), (2, 10, 0, 35), (2, 11, 2, 36), (2, 7, 1, 32),
-    (2, 10, 3, 34), (2, 7, 4, 33), (3, 8, 3, 38), (3, 18, 2, 43), (3, 9, 0, 39),
-    (3, 7, 5, 42), (3, 9, 1, 41), (3, 8, 4, 40), (4, 24, 2, 47), (4, 24, 0, 48),
-    (4, 24, 5, 46), (4, 23, 4, 45), (4, 24, 1, 49), (4, 23, 3, 44), (4, 13, 0, 50),
-    (4, 22, 1, 54), (4, 8, 5, 53), (4, 12, 3, 55), (4, 14, 4, 51), (4, 23, 0, 57),
-    (4, 14, 3, 56), (4, 14, 5, 61), (5, 27, 2, 52), (5, 27, 4, 59), (5, 26, 2, 58),
-    (5, 30, 1, 60), (6, 25, 3, 67), (6, 28, 2, 63), (6, 29, 1, 65), (6, 35, 4, 64),
-    (6, 26, 0, 62), (6, 25, 5, 66), (7, 29, 0, 72), (7, 28, 3, 69), (7, 31, 2, 73),
-    (7, 28, 4, 70), (7, 34, 1, 68), (7, 30, 5, 71), (8, 45, 4, 75), (8, 48, 0, 79),
-    (8, 46, 2, 76), (8, 46, 1, 78), (8, 48, 5, 77), (8, 45, 3, 74), (9, 47, 0, 83),
-    (9, 52, 4, 82), (9, 49, 2, 84), (9, 54, 5, 85), (9, 35, 3, 80), (9, 52, 1, 81),
-    (10, 42, 5, 90), (10, 59, 1, 88), (10, 31, 3, 91), (10, 58, 0, 86), (10, 59, 4, 89),
-    (10, 52, 2, 87), (11, 63, 0, 92), (11, 66, 2, 96), (11, 66, 3, 97), (11, 65, 1, 94),
-    (11, 64, 4, 93), (11, 66, 5, 95), (12, 68, 4, 100), (12, 54, 1, 103), (12, 63, 2, 98),
-    (12, 71, 5, 101), (12, 64, 3, 99), (12, 42, 0, 102), (13, 75, 3, 104), (13, 77, 0, 106),
-    (13, 77, 2, 105), (13, 75, 4, 107), (13, 76, 1, 108), (13, 60, 5, 109), (14, 84, 4, 114),
-    (14, 72, 3, 111), (14, 79, 2, 112), (14, 32, 5, 115), (14, 73, 0, 113), (14, 32, 1, 110),
-    (15, 89, 3, 121), (15, 88, 2, 118), (15, 33, 0, 116), (15, 87, 4, 119), (15, 87, 5, 117),
-    (15, 89, 1, 120), (16, 83, 4, 126), (16, 81, 5, 122), (16, 92, 2, 124), (16, 35, 0, 123),
-    (16, 93, 3, 125), (18, 108, 1, 127),
+    (0, 0, 5, 6), (0, 0, 6, 7), (0, 0, 11, 11), (0, 0, 12, 10), (0, 0, 10, 8),
+    (0, 0, 9, 9), (0, 0, 7, 12), (0, 0, 8, 17), (1, 4, 2, 13), (1, 5, 4, 15),
+    (1, 5, 0, 14), (1, 6, 5, 16), (1, 5, 3, 19), (1, 4, 1, 18), (1, 6, 2, 20),
+    (1, 6, 0, 21), (2, 7, 7, 25), (2, 11, 13, 31), (2, 7, 1, 24), (2, 8, 2, 22),
+    (2, 10, 0, 23), (2, 12, 0, 30), (2, 11, 1, 27), (2, 12, 5, 28), (2, 12, 3, 29),
+    (2, 10, 2, 26), (3, 14, 4, 35), (3, 17, 3, 33), (3, 16, 5, 36), (3, 15, 2, 34),
+    (3, 17, 1, 32), (3, 16, 0, 37), (3, 15, 3, 39), (3, 15, 4, 41), (3, 16, 2, 42),
+    (3, 7, 5, 43), (3, 8, 0, 38), (3, 15, 1, 40), (4, 24, 3, 49), (4, 23, 4, 46),
+    (4, 24, 2, 48), (4, 22, 5, 47), (4, 19, 1, 45), (4, 23, 0, 44), (5, 27, 4, 52),
+    (5, 25, 3, 55), (5, 25, 1, 54), (5, 26, 0, 50), (5, 11, 2, 51), (5, 25, 5, 53),
+    (6, 31, 3, 58), (6, 36, 5, 59), (6, 31, 2, 57), (6, 31, 4, 60), (6, 36, 0, 61),
+    (6, 31, 1, 56), (7, 37, 2, 66), (7, 29, 1, 67), (7, 35, 3, 63), (7, 32, 4, 62),
+    (7, 41, 0, 64), (7, 42, 5, 65), (8, 47, 5, 72), (8, 46, 4, 70), (8, 42, 1, 73),
+    (8, 46, 2, 68), (8, 46, 0, 69), (8, 36, 3, 71), (9, 53, 3, 78), (9, 50, 0, 74),
+    (9, 48, 2, 79), (9, 53, 1, 77), (9, 39, 4, 75), (9, 53, 5, 76), (10, 59, 0, 82),
+    (10, 48, 5, 85), (10, 60, 2, 84), (10, 56, 3, 81), (10, 56, 4, 83), (10, 57, 1, 80),
+    (11, 58, 3, 87), (11, 66, 5, 89), (11, 55, 1, 91), (11, 61, 0, 90), (11, 62, 4, 86),
+    (11, 65, 2, 88), (12, 68, 4, 93), (12, 59, 2, 94), (12, 61, 3, 96), (12, 68, 0, 92),
+    (12, 65, 1, 97), (12, 72, 5, 95), (13, 34, 2, 98), (13, 76, 0, 99), (13, 70, 4, 100),
+    (13, 78, 5, 102), (13, 77, 3, 103), (13, 76, 1, 101), (14, 83, 2, 109), (14, 75, 0, 107),
+    (14, 57, 5, 105), (14, 26, 1, 104), (14, 34, 4, 106), (14, 81, 3, 108), (15, 82, 3, 113),
+    (15, 45, 4, 110), (15, 88, 5, 112), (15, 90, 2, 114), (15, 36, 1, 115), (15, 87, 0, 111),
+    (16, 42, 2, 119), (16, 85, 3, 121), (16, 92, 0, 117), (16, 95, 5, 118), (16, 96, 4, 120),
+    (16, 33, 1, 116), (17, 9, 4, 123), (17, 102, 1, 124), (17, 7, 3, 127), (17, 20, 0, 125),
+    (17, 13, 5, 126), (17, 1, 2, 122),
 )
 ROWS = 112
 SENT = 107
@@ -149,6 +154,7 @@
     load_sem,
     pair_sem,
     red_sem,
+    ready_sem,
 ):
     vectors, own, length = data_ref.shape
     me = tuple(lax.axis_index(name) for name in PARAM)
@@ -195,9 +201,9 @@
             device_id_type=MESH,
         )
 
-    def forward_after(k):
+    def forward_after(k, near=True, far=True):
         for when, source, vector, target in COPIES:
-            if when == k:
+            if when == k and (near if vector < 6 else far):
                 copy(source, target, 1, (target - 1) // GROUP, beside[vector]).start()
 
     def forward_between(k, low, high):
@@ -241,7 +247,9 @@
     gat[0, pl.ds(104, 8), :] = folded
 
     pl.semaphore_wait(barrier, 7)
-    forward_after(0)
+    forward_after(0, far=False)
+    for where in beside[:6]:
+        pl.semaphore_signal(ready_sem, inc=1, device_id=where, device_id_type=MESH)
     for slot, offset in offsets.items():
         z, x, y = (
             lax.rem(pos + n - o, n) for pos, o, n in zip(me, offset, TORUS)
@@ -349,8 +357,10 @@
                 c, p, h = i // 8, i // 2 % 4, i % 2
                 acc[c, pl.ds(p * 16 + h * 8, 8), pl.ds(ft * LANES, LANES)] = value
 
-    for ft in range(3):
-        transpose_tile(ft)
+    transpose_tile(0)
+    pl.semaphore_wait(ready_sem, 6)
+    forward_after(0, near=False)
+    transpose_tile(1)
 
     @pl.loop(1, last)
     def _(k):
@@ -359,6 +369,7 @@
 
         @pl.when(k == 1)
         def _():
+            transpose_tile(2)
             transpose_tile(3)
 
         @pl.when(k == 2)
@@ -496,6 +507,7 @@
             pltpu.SemaphoreType.DMA((7,)),
             pltpu.SemaphoreType.DMA((2,)),
             pltpu.SemaphoreType.DMA((4,)),
+            pltpu.SemaphoreType.REGULAR,
         ],
         compiler_params=pltpu.CompilerParams(
             collective_id=0, has_side_effects=True, vmem_limit_bytes=VMEM_LIMIT

time: 54.2 us -> 53.8 us (level)
  no operation moved by 1% of the time
where the time goes in v4:
time: 53.8 us; the launch traced here: 53.7 us
  Pallas kernels  51.9 us (96%)
  local copies, waits for them, and re-layouts  1.17 us (2%)
  between operations  0.64 us (1%)
    pallas_call x1, Pallas kernels, body(): pl.pallas_call(kernel, out_shape=(pltpu.VMEM((vectors, points, length), F...  51.9 us
    unnamed x2, local copies, waits for them, and re-layouts  1.17 us

profile of v4, /device:TPU:1, one launch (start us, length us, event | category | flops | bytes accessed | tf_op | source)
XLA Modules:
  0.0 53.7 jit_solution(8783906855241174805)
XLA Ops:
  0.6 51.9 %adjoint.1 = (f32[16,4,420]{2,1,0:T(4,128)S(1)}, f32[16]{0:T(128)S(1)}) custom-call(f32[16,2,420]{2,1,0:T(2,128)} %data_ref.1, f32[2,3368,128]{2,1,0:T(8,128)} %bitcast.5, bf16[512,512]{1,0:T(8,128)(2,1)} %constant.10.clone.fh_ref, bf16[512,512]{1,0:T(8,128)(2,1)} %constant.11.clone.fl_ref, bf16[2,256,256]{2,1,0:T(8,128)(2,1)} %constant.12.clone.ah_ref, ...), custom_call_target="tpu_custom_call" | custom-call | tf_op jit(solution)/shard_map/adjoint/pallas_call | solution.py:478
  52.6 0.7 %copy.12 = f32[16,4,420]{2,1,0:T(4,128)} copy(f32[16,4,420]{2,1,0:T(4,128)S(1)} %get-tuple-element.2) | data formatting | bytes 215040
  53.2 0.5 copy.13

commit v5 on v4

--- a/solution.py
+++ b/solution.py
@@ -73,6 +73,10 @@
     return tuple((a + b) % n for a, b, n in zip(offset, step, TORUS))
 
 
+def hops(offset):
+    return sum(min(o, n - o) for o, n in zip(offset, TORUS))
+
+
 def spectral_tables(steps):
     half = steps // 2
     t = np.arange(steps)[:, None]
@@ -247,7 +251,10 @@
     gat[0, pl.ds(104, 8), :] = folded
 
     pl.semaphore_wait(barrier, 7)
-    forward_after(0, far=False)
+    @pl.when(core == 0)
+    def _():
+        forward_after(0, far=False)
+
     for where in beside[:6]:
         pl.semaphore_signal(ready_sem, inc=1, device_id=where, device_id_type=MESH)
     for slot, offset in offsets.items():
@@ -264,6 +271,10 @@
     loads[4].wait()
     loads[5].wait()
     loads[6].wait()
+
+    @pl.when(core == 1)
+    def _():
+        forward_after(0, far=False)
 
     def transpose_tile(ft):
         parity, half = divmod(ft, 2)
@@ -374,17 +385,17 @@
 
         @pl.when(k == 2)
         def _():
-            consume(0, 1)
-
-        low = jnp.where(k == 2, 0, k - 1)
-        high = jnp.where(k == 1, 0, k)
+            consume(0, 2)
+
+        low = jnp.maximum(k - 2, 0)
+        high = jnp.maximum(k - 1, 0)
 
         @pl.loop(low, high)
         def _(b):
-            consume(1 + GROUP * b, GROUP)
+            consume(2 + GROUP * b, GROUP)
 
     copy(0, GROUP * (last - 1) + 1, rest_of, last - 1, beside[0]).wait_recv()
-    consume(GROUP * (last - 1) + 1, rest_of)
+    consume(GROUP * (last - 2) + 2, GROUP)
 
     out_re = acc[0] * gain[0:1, :]
     out_im = acc[1] * gain[1:2, :]
@@ -437,15 +448,17 @@
         column = jnp.sum(square, axis=1, keepdims=True)
         red1[spot] = jnp.sum(jnp.where(diagonal, column, 0.0), axis=0, keepdims=True)
         peers = [(0, dx, dy) for dx in range(TORUS[1]) for dy in range(TORUS[2]) if dx + dy > 0]
+        peers.sort(key=hops, reverse=True)
         for offset in peers:
             message(red1, spot, 1, 0, device(offset)).start()
         message(red1, 0, len(peers), 0, beside[0]).wait()
         red2[z] = total_of(red1)
         line = [(dz, 0, 0) for dz in range(TORUS[0])]
-        for offset in line[1:]:
-            message(red2, z, 1, 2, device(offset)).start()
+        line.sort(key=hops, reverse=True)
         for offset in line:
             message(red2, z, 1, 2, dict(device(offset), sensor=0)).start()
+            if hops(offset) > 0:
+                message(red2, z, 1, 2, device(offset)).start()
         message(red2, 0, TORUS[0] - 1, 2, beside[0]).wait_recv()
         message(red1, 0, 2 * TORUS[0] - 1, 2, beside[0]).wait_send()
 

time: 53.8 us -> 53.7 us (level)
  no operation moved by 1% of the time
where the time goes in v5:
time: 53.7 us; the launch traced here: 53.6 us
  Pallas kernels  51.8 us (96%)
  local copies, waits for them, and re-layouts  1.17 us (2%)
  between operations  0.64 us (1%)
    pallas_call x1, Pallas kernels, body(): pl.pallas_call(kernel, out_shape=(pltpu.VMEM((vectors, points, length), F...  51.8 us
    unnamed x2, local copies, waits for them, and re-layouts  1.17 us

profile of v5, /device:TPU:1, one launch (start us, length us, event | category | flops | bytes accessed | tf_op | source)
XLA Modules:
  0.0 53.6 jit_solution(9838261199231955976)
XLA Ops:
  0.6 51.8 %adjoint.1 = (f32[16,4,420]{2,1,0:T(4,128)S(1)}, f32[16]{0:T(128)S(1)}) custom-call(f32[16,2,420]{2,1,0:T(2,128)} %data_ref.1, f32[2,3368,128]{2,1,0:T(8,128)} %bitcast.5, bf16[512,512]{1,0:T(8,128)(2,1)} %constant.10.clone.fh_ref, bf16[512,512]{1,0:T(8,128)(2,1)} %constant.11.clone.fl_ref, bf16[2,256,256]{2,1,0:T(8,128)(2,1)} %constant.12.clone.ah_ref, ...), custom_call_target="tpu_custom_call" | custom-call | tf_op jit(solution)/shard_map/adjoint/pallas_call | solution.py:491
  52.4 0.7 %copy.12 = f32[16,4,420]{2,1,0:T(4,128)} copy(f32[16,4,420]{2,1,0:T(4,128)S(1)} %get-tuple-element.2) | data formatting | bytes 215040
  53.1 0.5 copy.13

commit v6 on v5

--- a/solution.py
+++ b/solution.py
@@ -381,10 +381,10 @@
         @pl.when(k == 1)
         def _():
             transpose_tile(2)
-            transpose_tile(3)
 
         @pl.when(k == 2)
         def _():
+            transpose_tile(3)
             consume(0, 2)
 
         low = jnp.maximum(k - 2, 0)

time: 53.7 us -> 54.1 us (level)
  no operation moved by 1% of the time
where the time goes in v6:
time: 54.1 us; the launch traced here: 54 us
  Pallas kernels  52.2 us (96%)
  local copies, waits for them, and re-layouts  1.17 us (2%)
  between operations  0.64 us (1%)
    pallas_call x1, Pallas kernels, body(): pl.pallas_call(kernel, out_shape=(pltpu.VMEM((vectors, points, length), F...  52.2 us
    unnamed x2, local copies, waits for them, and re-layouts  1.17 us

profile of v6, /device:TPU:1, one launch (start us, length us, event | category | flops | bytes accessed | tf_op | source)
XLA Modules:
  0.0 54.0 jit_solution(3373478655858523596)
XLA Ops:
  0.6 52.2 %adjoint.1 = (f32[16,4,420]{2,1,0:T(4,128)S(1)}, f32[16]{0:T(128)S(1)}) custom-call(f32[16,2,420]{2,1,0:T(2,128)} %data_ref.1, f32[2,3368,128]{2,1,0:T(8,128)} %bitcast.5, bf16[512,512]{1,0:T(8,128)(2,1)} %constant.10.clone.fh_ref, bf16[512,512]{1,0:T(8,128)(2,1)} %constant.11.clone.fl_ref, bf16[2,256,256]{2,1,0:T(8,128)(2,1)} %constant.12.clone.ah_ref, ...), custom_call_target="tpu_custom_call" | custom-call | tf_op jit(solution)/shard_map/adjoint/pallas_call | solution.py:491
  52.8 0.7 %copy.12 = f32[16,4,420]{2,1,0:T(4,128)} copy(f32[16,4,420]{2,1,0:T(4,128)S(1)} %get-tuple-element.2) | data formatting | bytes 215040
  53.5 0.5 copy.13
